TPU v7x, 256 devices: a whole 4x4x8 slice. The times are simulated.
256 devices in a mesh: band: 64 (over z, y, core), field: 4 (over x).
Axes of the slice: x: 4, y: 4, z: 8, core: 2. Of those that a mesh axis runs over, the one named last changes fastest.
Arguments:
- right_side: float32 [640, 2, 4, 12, 640], P('band', None, 'field'), may hold values from -40 to 40
- legendre: bfloat16 [640, 640, 640], P('band'), may hold values from -0.25 to 0.25
- wave_map: int32 [640], replicated, may hold values from 0 to 639, as said below
- obs_weight: float32 [640, 1280], P('band'), may hold values from 0.2 to 5
Outputs:
- solution: float32 [640, 2, 4, 12, 640], P('band', None, 'field')
- residual: float32 [640, 2, 4, 12, 640], P('band', None, 'field')
Inputs may be any that keep to these rules, and one draw needn't show every extreme that they name: A permutation of 0 to 639; wave_map[s] lies in the same aligned block of 20 values as 639-s.
All inputs are finite; a program needn't handle non-finite values.
Results may differ from a plain program's by a relative error of at most 0.03.
Values may be sent and summed in bfloat16 or wider, within the bound.
No kernel may reach another device: no remote copies, remote signals or barrier semaphores. Data moves between devices by JAX's collectives and lax.ppermute only.
A program may use at most 128 MiB of HBM per device.

v0:
```python
import functools
import math
import jax
import jax.numpy as jnp
from jax import lax
from jax.sharding import Mesh
from jax.sharding import PartitionSpec as P

ITERS = 3
BAND_FIELD = ("band_0", "band_1", "band_2", "field")
BAND = ("band_0", "band_1", "band_2")


def by_axis(array, axes):
    return functools.reduce(lax.psum, axes, array)


def triangle_of(own_waves, degrees):
    return (jnp.arange(degrees, dtype=jnp.int32)[None, :] >= own_waves[:, None]).astype(jnp.float32)


def fourier_of(wave_map, lon_count):
    longitude = jnp.arange(lon_count, dtype=jnp.int32)
    phase_int = wave_map[:, None] * longitude[None, :] % lon_count
    angles = phase_int.astype(jnp.float32) * (2.0 * math.pi / lon_count)
    norm_factor = 1.0 / math.sqrt(wave_map.shape[0])
    return (jnp.stack([jnp.cos(angles), -jnp.sin(angles)], axis=1) * norm_factor).astype(
        jnp.bfloat16
    )


def grid_round(spread, fourier_flat, obs_weight):
    slots, parts, items, single, lat_rows = spread.shape
    flat = spread.reshape(slots * parts, items * single * lat_rows)
    grid_vals = lax.dot_general(
        flat, fourier_flat, (((0,), (0,)), ((), ())), preferred_element_type=jnp.float32
    )
    grid_vals = (
        grid_vals.reshape(items * single, lat_rows, fourier_flat.shape[1]) * obs_weight[None, :, :]
    )
    weighted = grid_vals.astype(jnp.bfloat16).reshape(
        items * single * lat_rows, fourier_flat.shape[1]
    )
    returned = lax.dot_general(
        fourier_flat, weighted, (((1,), (1,)), ((), ())), preferred_element_type=jnp.float32
    ).astype(jnp.bfloat16)
    return returned.reshape(slots, parts, items, single, lat_rows)


def legendre_back(returned, legendre):
    return lax.dot_general(
        returned, legendre, (((4,), (2,)), ((0,), (0,))), preferred_element_type=jnp.float32
    )


def paired_sums(residual, image_vec):
    return (
        by_axis(jnp.sum(residual * residual), BAND_FIELD),
        by_axis(jnp.sum(residual * image_vec), BAND_FIELD),
    )


def on_device(right_side, legendre, wave_map, obs_weight):
    slot_count = legendre.shape[0]
    band_count = lax.axis_size(BAND)
    lat_rows = obs_weight.shape[0]
    first_slot = lax.axis_index(BAND) * slot_count
    own_waves = lax.dynamic_slice_in_dim(wave_map, first_slot, slot_count)
    triangle = triangle_of(own_waves, right_side.shape[4])
    fourier_table = fourier_of(wave_map, obs_weight.shape[1])
    fourier_flat = fourier_table.reshape(2 * fourier_table.shape[0], fourier_table.shape[2])
    triangle_five = triangle[:, None, None, None, :]
    field_count = right_side.shape[2]
    level_count = right_side.shape[3]
    merged = field_count * level_count

    def operate(vector):
        masked_bf = (vector * triangle_five).astype(jnp.bfloat16)
        coeffs = lax.dot_general(
            masked_bf, legendre, (((4,), (1,)), ((0,), (0,))), preferred_element_type=jnp.float32
        ).astype(jnp.bfloat16)
        outgoing = coeffs.reshape(slot_count, 2, merged, band_count, lat_rows)
        spread = lax.all_to_all(outgoing, BAND, split_axis=3, concat_axis=0, tiled=True)
        returned = grid_round(spread, fourier_flat, obs_weight)
        returned_home = lax.all_to_all(returned, BAND, split_axis=0, concat_axis=3, tiled=True)
        home = returned_home.reshape(slot_count, 2, field_count, level_count, band_count * lat_rows)
        adjoint = legendre_back(home, legendre)
        return vector + triangle_five * adjoint

    residual = right_side * triangle_five
    solution = jnp.zeros_like(residual)
    image_vec = operate(residual)
    norm_now, product = paired_sums(residual, image_vec)
    step_length = norm_now / product
    direction = residual
    along = image_vec
    for iteration in range(ITERS):
        solution = solution + step_length * direction
        residual = residual - step_length * along
        if iteration + 1 < ITERS:
            image_vec = operate(residual)
            norm_next, product = paired_sums(residual, image_vec)
            beta_ratio = norm_next / norm_now
            step_length = norm_next / (product - beta_ratio * norm_next / step_length)
            direction = residual + beta_ratio * direction
            along = image_vec + beta_ratio * along
            norm_now = norm_next
    return (solution, residual)


def solution(mesh):
    split = Mesh(
        mesh.devices.reshape(8, 4, 2, mesh.shape["field"]), ("band_0", "band_1", "band_2", "field")
    )
    return jax.shard_map(
        on_device,
        mesh=split,
        in_specs=(P(BAND, None, "field", None, None), P(BAND, None, None), P(), P(BAND, None)),
        out_specs=(P(BAND, None, "field", None, None), P(BAND, None, "field", None, None)),
        check_vma=False,
    )
```

profile of v0, /device:TPU:32, one launch (start us, length us, event | category | flops | bytes accessed | tf_op | source)
XLA Modules:
  0.0 736.9 jit_solution(9783474237335254011)
XLA Ops:
  1.5 4.9 fusion.49
  6.4 9.7 %reshape.240 = bf16[10,2,12,64,10]{4,3,2,1,0:T(8,128)(2,1)} reshape(bf16[10,2,12,640]{3,2,1,0:T(8,128)(2,1)S(1)} %fusion.49) | data formatting | bytes 614400 | tf_op jit(solution)/shard_map/reshape | solution.py:82
  16.1 14.1 %copy.117 = bf16[10,2,12,64,10]{2,1,4,0,3:T(2,128)(2,1)S(1)} copy(bf16[10,2,12,64,10]{4,3,2,1,0:T(8,128)(2,1)} %reshape.240) | data formatting | bytes 614400 | tf_op jit(solution)/shard_map/reshape | solution.py:82
  30.2 4.4 reshape.247
  34.6 12.1 %all-to-all-start = ((bf16[64,2,1200]{2,1,0:T(2,128)(2,1)}), bf16[64,2,1200]{2,1,0:T(2,128)(2,1)}, u32[]{:S(2)}, u32[]{:S(2)}) async-start(bf16[64,2,1200]{2,1,0:T(2,128)(2,1)} %reshape.247), calls=%async_computation | async-start | bytes 655360 | tf_op jit(solution)/shard_map/all_to_all | solution.py:83
  46.7 13.8 %fusion.17 = (f32[640,1,1280]{2,0,1:T(8,128)S(1)}, f32[640,1,1280]{2,0,1:T(8,128)S(1)}) fusion(s32[640]{0:T(1024)S(1)} %copy-done.2), kind=kLoop, calls=%fused_computation.21 | loop fusion | flops 8192000 | bytes 6556160 | tf_op jit(solution)/shard_map/cos | solution.py:27
  71.2 7.8 %reshape.248 = bf16[64,10,10,2,12]{4,3,2,1,0:T(2,128)(2,1)S(1)} reshape(bf16[64,2,1200]{2,1,0:T(2,128)(2,1)} %all-to-all-done) | data formatting | bytes 614400
  79.0 4.0 bitcast_bitcast_fusion.2
  83.1 13.4 %copy.118 = bf16[64,10,2,12,1,10]{5,3,2,1,0,4:T(8,128)(2,1)} copy(bf16[64,10,2,12,1,10]{3,2,5,1,0,4:T(2,128)(2,1)} %bitcast_bitcast_fusion.2) | data formatting | bytes 614400 | tf_op jit(solution)/shard_map/all_to_all | solution.py:83
  96.4 6.4 reshape.222
  113.7 5.8 reshape.224
  119.5 12.1 %copy.123 = bf16[640,2,12,1,10]{2,1,4,3,0:T(2,128)(2,1)S(1)} copy(bf16[640,2,12,1,10]{4,2,1,0,3:T(8,128)(2,1)} %reshape.224) | data formatting | bytes 614400 | tf_op jit(solution)/shard_map/reshape | solution.py:47
  131.6 4.4 reshape.249
  136.0 23.7 %all_to_all.90 = bf16[64,2,1200]{2,1,0:T(2,128)(2,1)} all-to-all(bf16[64,2,1200]{2,1,0:T(2,128)(2,1)} %reshape.249), channel_id=1, replica_groups=mesh['band_0'=8,'band_1'=4,'band_2'=2,'field'=4] {'band_0','band_1','ban..., dimensions={0} | all-to-all | bytes 614400 | tf_op jit(solution)/shard_map/all_to_all | solution.py:85
  159.7 7.8 %reshape.250 = bf16[640,1,10,2,12]{4,3,2,1,0:T(2,128)(2,1)S(1)} reshape(bf16[64,2,1200]{2,1,0:T(2,128)(2,1)} %all_to_all.90) | data formatting | bytes 614400
  167.5 17.5 %copy.154 = bf16[64,10,2,12,1,10]{1,0,2,5,3,4:T(8,128)(2,1)} copy(bf16[64,10,2,12,1,10]{3,2,5,1,0,4:T(2,128)(2,1)S(1)} %bitcast.136) | data formatting | bytes 614400 | tf_op jit(solution)/shard_map/all_to_all | solution.py:85
  185.0 12.6 %copy.155 = bf16[10,2,12,64,1,10]{5,3,2,1,0,4:T(8,128)(2,1)} copy(bf16[10,2,12,64,1,10]{0,3,1,5,2,4:T(8,128)(2,1)} %bitcast.132) | data formatting | bytes 614400 | tf_op jit(solution)/shard_map/reshape.6
  197.7 6.7 reshape.242
  204.3 6.5 fusion.66
  210.8 16.0 %all-reduce.2 = (f32[]{:T(128)}, f32[]{:T(128)}) all-reduce(f32[]{:T(128)} %get-tuple-element.17, f32[]{:T(128)} %get-tuple-element.16), channel_id=1, replica_groups=mesh['band_0'=8,'band_1'=4,'band_2'=2,'field'=4] {'band_0'}, use_global_device_ids=true, to_apply=%region_1.2 | all-reduce | flops 2 | bytes 16 | tf_op jit(solution)/shard_map/psum | solution.py:15
  226.8 10.6 %all-reduce.8 = (f32[]{:T(128)}, f32[]{:T(128)}) all-reduce(f32[]{:T(128)} %get-tuple-element.22, f32[]{:T(128)} %get-tuple-element.23), channel_id=1, replica_groups=mesh['band_0'=8,'band_1'=4,'band_2'=2,'field'=4] {'band_1'}, use_global_device_ids=true, to_apply=%region_2.3 | all-reduce | flops 2 | bytes 16 | tf_op jit(solution)/shard_map/psum | solution.py:15
  240.5 11.4 %all-reduce.5 = (f32[]{:T(128)}, f32[]{:T(128)}) all-reduce(f32[]{:T(128)} %get-tuple-element.40, f32[]{:T(128)} %get-tuple-element.41), channel_id=1, replica_groups=mesh['band_0'=8,'band_1'=4,'band_2'=2,'field'=4] {'field'}, use_global_device_ids=true, to_apply=%region_4.5 | all-reduce | flops 2 | bytes 16 | tf_op jit(solution)/shard_map/psum | solution.py:15
  253.4 4.7 fusion.52
  258.1 9.7 %reshape.243 = bf16[10,2,12,64,10]{4,3,2,1,0:T(8,128)(2,1)} reshape(bf16[10,2,12,640]{3,2,1,0:T(8,128)(2,1)S(1)} %fusion.52) | data formatting | bytes 614400 | tf_op jit(solution)/shard_map/reshape | solution.py:82
  267.8 14.6 %copy.128 = bf16[10,2,12,64,10]{2,1,4,0,3:T(2,128)(2,1)} copy(bf16[10,2,12,64,10]{4,3,2,1,0:T(8,128)(2,1)} %reshape.243) | data formatting | bytes 614400 | tf_op jit(solution)/shard_map/reshape | solution.py:82
  282.4 7.0 reshape.251
  289.4 19.6 %all_to_all.91 = bf16[64,2,1200]{2,1,0:T(2,128)(2,1)S(1)} all-to-all(bf16[64,2,1200]{2,1,0:T(2,128)(2,1)S(1)} %reshape.251), channel_id=1, replica_groups=mesh['band_0'=8,'band_1'=4,'band_2'=2,'field'=4] {'band_0','band_1','ban..., dimensions={0} | all-to-all | bytes 614400 | tf_op jit(solution)/shard_map/all_to_all | solution.py:83
  309.0 3.9 reshape.252
  312.9 5.9 bitcast_bitcast_fusion.1
  318.8 13.2 %copy.129 = bf16[64,10,2,12,1,10]{5,3,2,1,0,4:T(8,128)(2,1)} copy(bf16[64,10,2,12,1,10]{3,2,5,1,0,4:T(2,128)(2,1)} %bitcast_bitcast_fusion.1) | data formatting | bytes 614400 | tf_op jit(solution)/shard_map/all_to_all | solution.py:83
  332.0 6.4 reshape.228
  347.5 5.7 reshape.230
  353.3 12.7 %copy.134 = bf16[640,2,12,1,10]{2,1,4,3,0:T(2,128)(2,1)} copy(bf16[640,2,12,1,10]{4,2,1,0,3:T(8,128)(2,1)} %reshape.230) | data formatting | bytes 614400 | tf_op jit(solution)/shard_map/reshape | solution.py:47
  365.9 7.0 reshape.253
  372.9 19.2 %all_to_all.92 = bf16[64,2,1200]{2,1,0:T(2,128)(2,1)S(1)} all-to-all(bf16[64,2,1200]{2,1,0:T(2,128)(2,1)S(1)} %reshape.253), channel_id=1, replica_groups=mesh['band_0'=8,'band_1'=4,'band_2'=2,'field'=4] {'band_0','band_1','ban..., dimensions={0} | all-to-all | bytes 614400 | tf_op jit(solution)/shard_map/all_to_all | solution.py:85
  392.1 3.9 reshape.254
  396.0 15.4 %copy.158 = bf16[64,10,2,12,1,10]{1,0,2,5,3,4:T(8,128)(2,1)} copy(bf16[64,10,2,12,1,10]{3,2,5,1,0,4:T(2,128)(2,1)} %bitcast.138) | data formatting | bytes 614400 | tf_op jit(solution)/shard_map/all_to_all | solution.py:85
  411.4 12.6 %copy.159 = bf16[10,2,12,64,1,10]{5,3,2,1,0,4:T(8,128)(2,1)} copy(bf16[10,2,12,64,1,10]{0,3,1,5,2,4:T(8,128)(2,1)} %bitcast.133) | data formatting | bytes 614400 | tf_op jit(solution)/shard_map/reshape.12
  424.1 6.6 reshape.244
  430.7 7.4 %multiply_reduce_fusion.2 = (f32[]{:T(128)}, f32[]{:T(128)}, f32[10,2,1,12,640]{4,3,1,0,2:T(8,128)}) fusion(f32[10,2,1,12,640]{4,3,1,0,2:T(8,128)S(1)} %fusion.59, bf16[10,2,12,640]{3,2,1,0:T(8,128)(2,1)S(1)} %reshape.244, bf16[10,640,640]{2,1,0:T(8,128)(2,1)} %param.5, f32[10,640]{1,0:T(8,128)S(1)} %fusion.82), kind=kOutput, calls=%fused_computation.63 | convolution fusion | flops 197529600 | bytes 9753608 | tf_op jit(solution)/shard_map/dot_general | solution.py:51
  438.2 16.1 %all-reduce.1 = (f32[]{:T(128)}, f32[]{:T(128)}) all-reduce(f32[]{:T(128)} %get-tuple-element.15, f32[]{:T(128)} %get-tuple-element.14), channel_id=1, replica_groups=mesh['band_0'=8,'band_1'=4,'band_2'=2,'field'=4] {'band_0'}, use_global_device_ids=true, to_apply=%region_11.12 | all-reduce | flops 2 | bytes 16 | tf_op jit(solution)/shard_map/psum | solution.py:15
  454.2 10.6 %all-reduce.7 = (f32[]{:T(128)}, f32[]{:T(128)}) all-reduce(f32[]{:T(128)} %get-tuple-element.20, f32[]{:T(128)} %get-tuple-element.21), channel_id=1, replica_groups=mesh['band_0'=8,'band_1'=4,'band_2'=2,'field'=4] {'band_1'}, use_global_device_ids=true, to_apply=%region_12.13 | all-reduce | flops 2 | bytes 16 | tf_op jit(solution)/shard_map/psum | solution.py:15
  468.0 8.4 %all-reduce.4 = (f32[]{:T(128)}, f32[]{:T(128)}) all-reduce(f32[]{:T(128)} %get-tuple-element.38, f32[]{:T(128)} %get-tuple-element.39), channel_id=1, replica_groups=mesh['band_0'=8,'band_1'=4,'band_2'=2,'field'=4] {'field'}, use_global_device_ids=true, to_apply=%region_14.15 | all-reduce | flops 2 | bytes 16 | tf_op jit(solution)/shard_map/psum | solution.py:15
  482.2 5.5 fusion.55
  487.7 10.4 %reshape.245 = bf16[10,2,12,64,10]{4,3,2,1,0:T(8,128)(2,1)} reshape(bf16[10,2,12,640]{3,2,1,0:T(8,128)(2,1)} %fusion.55) | data formatting | bytes 614400 | tf_op jit(solution)/shard_map/reshape | solution.py:82
  498.1 14.6 %copy.139 = bf16[10,2,12,64,10]{2,1,4,0,3:T(2,128)(2,1)} copy(bf16[10,2,12,64,10]{4,3,2,1,0:T(8,128)(2,1)} %reshape.245) | data formatting | bytes 614400 | tf_op jit(solution)/shard_map/reshape | solution.py:82
  512.6 7.6 %reshape.255 = bf16[64,2,1200]{2,1,0:T(2,128)(2,1)} reshape(bf16[64,10,10,2,12]{4,3,2,1,0:T(2,128)(2,1)} %bitcast.139) | data formatting | bytes 614400
  520.3 19.6 %all_to_all.93 = bf16[64,2,1200]{2,1,0:T(2,128)(2,1)} all-to-all(bf16[64,2,1200]{2,1,0:T(2,128)(2,1)} %reshape.255), channel_id=1, replica_groups=mesh['band_0'=8,'band_1'=4,'band_2'=2,'field'=4] {'band_0','band_1','ban..., dimensions={0} | all-to-all | bytes 614400 | tf_op jit(solution)/shard_map/all_to_all | solution.py:83
  539.9 8.6 %reshape.256 = bf16[64,10,10,2,12]{4,3,2,1,0:T(2,128)(2,1)} reshape(bf16[64,2,1200]{2,1,0:T(2,128)(2,1)} %all_to_all.93) | data formatting | bytes 614400
  548.5 5.9 bitcast_bitcast_fusion
  554.4 13.2 %copy.140 = bf16[64,10,2,12,1,10]{5,3,2,1,0,4:T(8,128)(2,1)} copy(bf16[64,10,2,12,1,10]{3,2,5,1,0,4:T(2,128)(2,1)} %bitcast_bitcast_fusion) | data formatting | bytes 614400 | tf_op jit(solution)/shard_map/all_to_all | solution.py:83
  567.7 7.1 reshape.234
  589.7 6.7 reshape.236
  596.3 12.7 %copy.145 = bf16[640,2,12,1,10]{2,1,4,3,0:T(2,128)(2,1)} copy(bf16[640,2,12,1,10]{4,2,1,0,3:T(8,128)(2,1)} %reshape.236) | data formatting | bytes 614400 | tf_op jit(solution)/shard_map/reshape | solution.py:47
  609.0 7.6 %reshape.257 = bf16[64,2,1200]{2,1,0:T(2,128)(2,1)} reshape(bf16[640,1,10,2,12]{4,3,2,1,0:T(2,128)(2,1)} %bitcast.143) | data formatting | bytes 614400
  616.6 19.6 %all_to_all.94 = bf16[64,2,1200]{2,1,0:T(2,128)(2,1)} all-to-all(bf16[64,2,1200]{2,1,0:T(2,128)(2,1)} %reshape.257), channel_id=1, replica_groups=mesh['band_0'=8,'band_1'=4,'band_2'=2,'field'=4] {'band_0','band_1','ban..., dimensions={0} | all-to-all | bytes 614400 | tf_op jit(solution)/shard_map/all_to_all | solution.py:85
  636.2 8.6 %reshape.258 = bf16[640,1,10,2,12]{4,3,2,1,0:T(2,128)(2,1)} reshape(bf16[64,2,1200]{2,1,0:T(2,128)(2,1)} %all_to_all.94) | data formatting | bytes 614400
  644.8 15.4 %copy.162 = bf16[64,10,2,12,1,10]{1,0,2,5,3,4:T(8,128)(2,1)} copy(bf16[64,10,2,12,1,10]{3,2,5,1,0,4:T(2,128)(2,1)} %bitcast.140) | data formatting | bytes 614400 | tf_op jit(solution)/shard_map/all_to_all | solution.py:85
  660.3 12.7 %copy.163 = bf16[10,2,12,64,1,10]{5,3,2,1,0,4:T(8,128)(2,1)} copy(bf16[10,2,12,64,1,10]{0,3,1,5,2,4:T(8,128)(2,1)} %bitcast.134) | data formatting | bytes 614400 | tf_op jit(solution)/shard_map/reshape.18
  672.9 7.3 reshape.246
  680.2 7.6 %multiply_reduce_fusion = (f32[]{:T(128)}, f32[]{:T(128)}, f32[10,2,1,12,640]{4,3,1,0,2:T(8,128)}) fusion(f32[10,2,1,12,640]{4,3,1,0,2:T(8,128)S(1)} %multiply_subtract_fusion.1, bf16[10,2,12,640]{3,2,1,0:T(8,128)(2,1)} %reshape.246, bf16[10,640,640]{2,1,0:T(8,128)(2,1)} %param.5, f32[10,640]{1,0:T(8,128)S(1)} %fusion.82), kind=kOutput, calls=%fused_computation.58 | convolution fusion | flops 197529600 | bytes 9753608 | tf_op jit(solution)/shard_map/dot_general | solution.py:51
  687.8 16.0 %all-reduce = (f32[]{:T(128)}, f32[]{:T(128)}) all-reduce(f32[]{:T(128)} %get-tuple-element.13, f32[]{:T(128)} %get-tuple-element.12), channel_id=1, replica_groups=mesh['band_0'=8,'band_1'=4,'band_2'=2,'field'=4] {'band_0'}, use_global_device_ids=true, to_apply=%region_21.22 | all-reduce | flops 2 | bytes 16 | tf_op jit(solution)/shard_map/psum | solution.py:15
  703.8 10.6 %all-reduce.6 = (f32[]{:T(128)}, f32[]{:T(128)}) all-reduce(f32[]{:T(128)} %get-tuple-element.18, f32[]{:T(128)} %get-tuple-element.19), channel_id=1, replica_groups=mesh['band_0'=8,'band_1'=4,'band_2'=2,'field'=4] {'band_1'}, use_global_device_ids=true, to_apply=%region_22.23 | all-reduce | flops 2 | bytes 16 | tf_op jit(solution)/shard_map/psum | solution.py:15
  717.4 10.3 %all-reduce.3 = (f32[]{:T(128)}, f32[]{:T(128)}) all-reduce(f32[]{:T(128)} %get-tuple-element.36, f32[]{:T(128)} %get-tuple-element.37), channel_id=1, replica_groups=mesh['band_0'=8,'band_1'=4,'band_2'=2,'field'=4] {'field'}, use_global_device_ids=true, to_apply=%region_24.25 | all-reduce | flops 2 | bytes 16 | tf_op jit(solution)/shard_map/psum | solution.py:15
  (44 shorter events, 61.9 us)
Async XLA Ops:
  30.2 16.6 %copy-start.2 = (s32[640]{0:T(1024)S(1)}, s32[640]{0:T(1024)}, u32[]{:S(2)}) copy-start(s32[640]{0:T(1024)} %param.6) | copy-start | bytes 7684
  34.6 36.6 %all-to-all-start = ((bf16[64,2,1200]{2,1,0:T(2,128)(2,1)}), bf16[64,2,1200]{2,1,0:T(2,128)(2,1)}, u32[]{:S(2)}, u32[]{:S(2)}) async-start(bf16[64,2,1200]{2,1,0:T(2,128)(2,1)} %reshape.247), calls=%async_computation | async-start | bytes 655360 | tf_op jit(solution)/shard_map/all_to_all | solution.py:83
  96.4 7.5 %copy-start.3 = (f32[10,1280]{1,0:T(8,128)S(1)}, f32[10,1280]{1,0:T(8,128)}, u32[]{:S(2)}) copy-start(f32[10,1280]{1,0:T(8,128)} %param.7) | copy-start | bytes 153604
  103.9 5.7 copy-start.1
  197.6 6.7 copy-start
where the time goes:
time: 747 us; the launch traced here: 737 us
  local copies, waits for them, and re-layouts  419 us (56%)
  blocking collectives  221 us (30%)
  matrix products  55.6 us (7%)
  other arithmetic  18 us (2%)
  starting transfers between devices  12.1 us (2%)
  between operations  11.1 us (1%)
    psum x12, blocking collectives, by_axis(): return functools.reduce(lax.psum, axes, array)  119 us
    unnamed x22, local copies, waits for them, and re-layouts  81.6 us
    reshape x6, local copies, waits for them, and re-layouts, operate(): outgoing = coeffs.reshape(slot_count, 2, merged, band_count, lat_rows)  73.1 us
    all_to_all x3, blocking collectives, operate(): lax.all_to_all(returned, BAND, split_axis=0, concat_axis=3, tiled=True)  62.5 us
    another operation x6, local copies, waits for them, and re-layouts  58.5 us
    all_to_all x6, local copies, waits for them, and re-layouts, operate(): lax.all_to_all(outgoing, BAND, split_axis=3, concat_axis=0, tiled=True)  55.7 us
    reshape x6, local copies, waits for them, and re-layouts, grid_round(): return returned.reshape(slots, parts, items, single, lat_rows)  55.6 us
    all_to_all x3, local copies, waits for them, and re-layouts, operate(): lax.all_to_all(returned, BAND, split_axis=0, concat_axis=3, tiled=True)  48.3 us
  transfers between devices with their start and end apart: 1, of which 0 were waited for; matrix products, arithmetic and copies ran while one was open for 3% of the time, Pallas kernels for 0%

commit v1 on v0

--- a/solution.py
+++ b/solution.py
@@ -82,7 +82,10 @@
         outgoing = coeffs.reshape(slot_count, 2, merged, band_count, lat_rows)
         spread = lax.all_to_all(outgoing, BAND, split_axis=3, concat_axis=0, tiled=True)
         returned = grid_round(spread, fourier_flat, obs_weight)
-        returned_home = lax.all_to_all(returned, BAND, split_axis=0, concat_axis=3, tiled=True)
+        peers = lax.axis_size(BAND)
+        tiles = jnp.stack(jnp.split(returned, peers, axis=0), axis=0)
+        tiles = lax.all_to_all(tiles, BAND, split_axis=0, concat_axis=0)
+        returned_home = jnp.concatenate(tiles, axis=3)
         home = returned_home.reshape(slot_count, 2, field_count, level_count, band_count * lat_rows)
         adjoint = legendre_back(home, legendre)
         return vector + triangle_five * adjoint

time: 747 us -> 1100 us (1.47)
  local copies, waits for them, and re-layouts: 419 us -> 765 us
    unnamed x22 -> x381, local copies, waits for them, and re-layouts: 81.6 us -> 243 us
    another operation x6 -> x204, local copies, waits for them, and re-layouts: 58.5 us -> 217 us  [the longest x198 152 us: operate(): tiles = jnp.stack(jnp.split(returned, peers, axis=0), axis=0)]
    split x0 -> x204, local copies, waits for them, and re-layouts: none -> 114 us  [operate(): tiles = jnp.stack(jnp.split(returned, peers, axis=0), axis=0)]
    all_to_all x3 -> x0, local copies, waits for them, and re-layouts: 48.3 us -> none  [operate(): lax.all_to_all(returned, BAND, split_axis=0, concat_axis=3, tiled=True)]
    reshape x6 -> x3, local copies, waits for them, and re-layouts: 55.6 us -> 15.7 us  [operate(): returned_home = jnp.concatenate(tiles, axis=3)]
  transfers between devices with their start and end apart: 1 -> 1, of which waited for: 0 -> 0; matrix products, arithmetic and copies ran while one was open for 3% -> 2% of each run, Pallas kernels for 0% -> 0%
where the time goes in v1:
time: 1100 us; the launch traced here: 1080 us
  local copies, waits for them, and re-layouts  765 us (70%)
  blocking collectives  220 us (20%)
  matrix products  53.2 us (5%)
  other arithmetic  17.8 us (2%)
  starting transfers between devices  12.1 us (1%)
  between operations  12 us (1%)
    unnamed x381, local copies, waits for them, and re-layouts  243 us
    another operation x198, local copies, waits for them, and re-layouts, operate(): tiles = jnp.stack(jnp.split(returned, peers, axis=0), axis=0)  152 us
    psum x12, blocking collectives, by_axis(): return functools.reduce(lax.psum, axes, array)  119 us
    split x204, local copies, waits for them, and re-layouts, operate(): tiles = jnp.stack(jnp.split(returned, peers, axis=0), axis=0)  114 us
    reshape x6, local copies, waits for them, and re-layouts, operate(): outgoing = coeffs.reshape(slot_count, 2, merged, band_count, lat_rows)  73 us
    another operation x6, local copies, waits for them, and re-layouts  64.8 us
    all_to_all x3, blocking collectives, operate(): tiles = lax.all_to_all(tiles, BAND, split_axis=0, concat_axis=0)  61.9 us
    all_to_all x6, local copies, waits for them, and re-layouts, operate(): lax.all_to_all(outgoing, BAND, split_axis=3, concat_axis=0, tiled=True)  55.7 us
  transfers between devices with their start and end apart: 1, of which 0 were waited for; matrix products, arithmetic and copies ran while one was open for 2% of the time, Pallas kernels for 0%

profile of v1, /device:TPU:32, one launch (start us, length us, event | category | flops | bytes accessed | tf_op | source)
XLA Modules:
  0.0 1079.9 jit_solution(12090406999082745719)
XLA Ops:
  1.5 4.9 fusion.49
  6.4 9.7 reshape.621
  16.1 14.1 %copy.1089 = bf16[10,2,12,64,10]{2,1,4,0,3:T(2,128)(2,1)S(1)} copy(bf16[10,2,12,64,10]{4,3,2,1,0:T(8,128)(2,1)} %reshape.621) | data formatting | bytes 614400 | tf_op jit(solution)/shard_map/reshape | solution.py:82
  30.2 4.4 reshape.628
  34.6 12.1 %all-to-all-start = ((bf16[64,2,1200]{2,1,0:T(2,128)(2,1)}), bf16[64,2,1200]{2,1,0:T(2,128)(2,1)}, u32[]{:S(2)}, u32[]{:S(2)}) async-start(bf16[64,2,1200]{2,1,0:T(2,128)(2,1)} %reshape.628), calls=%async_computation | async-start | bytes 655360 | tf_op jit(solution)/shard_map/all_to_all | solution.py:83
  46.7 13.6 %fusion.17 = (f32[640,1,1280]{2,0,1:T(8,128)S(1)}, f32[640,1,1280]{2,0,1:T(8,128)S(1)}) fusion(s32[640]{0:T(1024)S(1)} %copy-done.85), kind=kLoop, calls=%fused_computation.21 | loop fusion | flops 8192000 | bytes 6556160 | tf_op jit(solution)/shard_map/cos | solution.py:27
  61.0 3.4 copy.1087
  64.4 3.3 reshape.620
  67.7 3.3 convert_element_type.96
  71.0 7.8 reshape.629
  78.9 3.9 bitcast_bitcast_fusion.5
  82.8 13.6 %copy.1090 = bf16[64,10,2,12,1,10]{5,3,2,1,0,4:T(8,128)(2,1)} copy(bf16[64,10,2,12,1,10]{3,2,5,1,0,4:T(2,128)(2,1)} %bitcast_bitcast_fusion.5) | data formatting | bytes 614400 | tf_op jit(solution)/shard_map/all_to_all | solution.py:83
  96.4 7.1 reshape.603
  200.0 14.6 %copy.1158 = bf16[64,10,2,12,1,10]{3,2,5,4,1,0:T(2,128)(2,1)S(1)} copy(bf16[64,10,2,12,1,10]{5,3,2,1,4,0:T(8,128)(2,1)} %constant_dynamic-update-slice_fusion) | data formatting | bytes 614400 | tf_op jit(solution)/shard_map/stack | solution.py:86
  214.6 4.6 reshape.630
  219.2 23.5 %all_to_all.60 = bf16[64,2,1200]{2,1,0:T(2,128)(2,1)} all-to-all(bf16[64,2,1200]{2,1,0:T(2,128)(2,1)} %reshape.630), channel_id=1, replica_groups=mesh['band_0'=8,'band_1'=4,'band_2'=2,'field'=4] {'band_0','band_1','ban..., dimensions={0} | all-to-all | bytes 614400 | tf_op jit(solution)/shard_map/all_to_all | solution.py:87
  242.7 7.8 reshape.631
  250.5 3.9 bitcast_bitcast_fusion.4
  254.5 14.8 %copy.1312 = bf16[10,2,12,64,1,10]{5,3,2,1,0,4:T(8,128)(2,1)} copy(bf16[10,2,12,64,1,10]{2,1,5,4,0,3:T(2,128)(2,1)} %bitcast_bitcast_fusion.4) | data formatting | bytes 614400 | tf_op jit(solution)/shard_map/reshape.154
  269.3 6.6 reshape.623
  275.9 6.5 fusion.66
  282.4 16.0 %all-reduce.2 = (f32[]{:T(128)}, f32[]{:T(128)}) all-reduce(f32[]{:T(128)} %get-tuple-element.19, f32[]{:T(128)} %get-tuple-element.18), channel_id=1, replica_groups=mesh['band_0'=8,'band_1'=4,'band_2'=2,'field'=4] {'band_0'}, use_global_device_ids=true, to_apply=%region_1.2 | all-reduce | flops 2 | bytes 16 | tf_op jit(solution)/shard_map/psum | solution.py:15
  298.4 10.6 all-reduce.8
  312.0 11.3 %all-reduce.5 = (f32[]{:T(128)}, f32[]{:T(128)}) all-reduce(f32[]{:T(128)} %get-tuple-element.42, f32[]{:T(128)} %get-tuple-element.43), channel_id=1, replica_groups=mesh['band_0'=8,'band_1'=4,'band_2'=2,'field'=4] {'field'}, use_global_device_ids=true, to_apply=%region_4.5 | all-reduce | flops 2 | bytes 16 | tf_op jit(solution)/shard_map/psum | solution.py:15
  324.7 4.7 fusion.52
  329.4 9.7 reshape.624
  339.2 14.6 %copy.1162 = bf16[10,2,12,64,10]{2,1,4,0,3:T(2,128)(2,1)} copy(bf16[10,2,12,64,10]{4,3,2,1,0:T(8,128)(2,1)} %reshape.624) | data formatting | bytes 614400 | tf_op jit(solution)/shard_map/reshape | solution.py:82
  353.7 7.0 reshape.632
  360.7 19.1 %all_to_all.61 = bf16[64,2,1200]{2,1,0:T(2,128)(2,1)S(1)} all-to-all(bf16[64,2,1200]{2,1,0:T(2,128)(2,1)S(1)} %reshape.632), channel_id=1, replica_groups=mesh['band_0'=8,'band_1'=4,'band_2'=2,'field'=4] {'band_0','band_1','ban..., dimensions={0} | all-to-all | bytes 614400 | tf_op jit(solution)/shard_map/all_to_all | solution.py:83
  379.8 3.9 reshape.633
  383.7 5.9 bitcast_bitcast_fusion.3
  389.6 13.2 %copy.1163 = bf16[64,10,2,12,1,10]{5,3,2,1,0,4:T(8,128)(2,1)} copy(bf16[64,10,2,12,1,10]{3,2,5,1,0,4:T(2,128)(2,1)} %bitcast_bitcast_fusion.3) | data formatting | bytes 614400 | tf_op jit(solution)/shard_map/all_to_all | solution.py:83
  402.8 6.8 reshape.609
  556.5 13.2 %copy.1231 = bf16[64,10,2,12,1,10]{3,2,5,4,1,0:T(2,128)(2,1)} copy(bf16[64,10,2,12,1,10]{5,3,2,1,4,0:T(8,128)(2,1)} %constant_dynamic-update-slice_fusion.64) | data formatting | bytes 614400 | tf_op jit(solution)/shard_map/stack | solution.py:86
  569.7 7.2 reshape.634
  576.9 19.0 %all_to_all.62 = bf16[64,2,1200]{2,1,0:T(2,128)(2,1)S(1)} all-to-all(bf16[64,2,1200]{2,1,0:T(2,128)(2,1)S(1)} %reshape.634), channel_id=1, replica_groups=mesh['band_0'=8,'band_1'=4,'band_2'=2,'field'=4] {'band_0','band_1','ban..., dimensions={0} | all-to-all | bytes 614400 | tf_op jit(solution)/shard_map/all_to_all | solution.py:87
  595.9 3.9 reshape.635
  599.8 5.9 bitcast_bitcast_fusion.2
  605.7 14.7 %copy.1315 = bf16[10,2,12,64,1,10]{5,3,2,1,0,4:T(8,128)(2,1)} copy(bf16[10,2,12,64,1,10]{2,1,5,4,0,3:T(2,128)(2,1)} %bitcast_bitcast_fusion.2) | data formatting | bytes 614400 | tf_op jit(solution)/shard_map/reshape.287
  620.4 6.6 reshape.625
  627.1 7.4 multiply_reduce_fusion.2
  634.5 16.0 %all-reduce.1 = (f32[]{:T(128)}, f32[]{:T(128)}) all-reduce(f32[]{:T(128)} %get-tuple-element.17, f32[]{:T(128)} %get-tuple-element.16), channel_id=1, replica_groups=mesh['band_0'=8,'band_1'=4,'band_2'=2,'field'=4] {'band_0'}, use_global_device_ids=true, to_apply=%region_11.12 | all-reduce | flops 2 | bytes 16 | tf_op jit(solution)/shard_map/psum | solution.py:15
  650.5 10.6 all-reduce.7
  664.1 8.6 all-reduce.4
  678.5 5.5 fusion.55
  684.0 10.4 reshape.626
  694.4 14.6 %copy.1235 = bf16[10,2,12,64,10]{2,1,4,0,3:T(2,128)(2,1)} copy(bf16[10,2,12,64,10]{4,3,2,1,0:T(8,128)(2,1)} %reshape.626) | data formatting | bytes 614400 | tf_op jit(solution)/shard_map/reshape | solution.py:82
  708.9 7.6 reshape.636
  716.5 19.4 %all_to_all.63 = bf16[64,2,1200]{2,1,0:T(2,128)(2,1)} all-to-all(bf16[64,2,1200]{2,1,0:T(2,128)(2,1)} %reshape.636), channel_id=1, replica_groups=mesh['band_0'=8,'band_1'=4,'band_2'=2,'field'=4] {'band_0','band_1','ban..., dimensions={0} | all-to-all | bytes 614400 | tf_op jit(solution)/shard_map/all_to_all | solution.py:83
  735.9 8.6 reshape.637
  744.6 5.9 bitcast_bitcast_fusion.1
  750.4 13.2 %copy.1236 = bf16[64,10,2,12,1,10]{5,3,2,1,0,4:T(8,128)(2,1)} copy(bf16[64,10,2,12,1,10]{3,2,5,1,0,4:T(2,128)(2,1)} %bitcast_bitcast_fusion.1) | data formatting | bytes 614400 | tf_op jit(solution)/shard_map/all_to_all | solution.py:83
  763.7 7.5 reshape.615
  946.5 13.2 %copy.1304 = bf16[64,10,2,12,1,10]{3,2,5,4,1,0:T(2,128)(2,1)} copy(bf16[64,10,2,12,1,10]{5,3,2,1,4,0:T(8,128)(2,1)} %constant_dynamic-update-slice_fusion.128) | data formatting | bytes 614400 | tf_op jit(solution)/shard_map/stack | solution.py:86
  959.8 7.8 reshape.638
  967.5 19.3 %all_to_all.64 = bf16[64,2,1200]{2,1,0:T(2,128)(2,1)} all-to-all(bf16[64,2,1200]{2,1,0:T(2,128)(2,1)} %reshape.638), channel_id=1, replica_groups=mesh['band_0'=8,'band_1'=4,'band_2'=2,'field'=4] {'band_0','band_1','ban..., dimensions={0} | all-to-all | bytes 614400 | tf_op jit(solution)/shard_map/all_to_all | solution.py:87
  986.9 8.6 reshape.639
  995.5 5.9 bitcast_bitcast_fusion
  1001.3 14.7 %copy.1318 = bf16[10,2,12,64,1,10]{5,3,2,1,0,4:T(8,128)(2,1)} copy(bf16[10,2,12,64,1,10]{2,1,5,4,0,3:T(2,128)(2,1)} %bitcast_bitcast_fusion) | data formatting | bytes 614400 | tf_op jit(solution)/shard_map/reshape.420
  1016.1 7.3 reshape.627
  1023.3 7.6 multiply_reduce_fusion
  1030.9 16.0 %all-reduce = (f32[]{:T(128)}, f32[]{:T(128)}) all-reduce(f32[]{:T(128)} %get-tuple-element.15, f32[]{:T(128)} %get-tuple-element.14), channel_id=1, replica_groups=mesh['band_0'=8,'band_1'=4,'band_2'=2,'field'=4] {'band_0'}, use_global_device_ids=true, to_apply=%region_21.22 | all-reduce | flops 2 | bytes 16 | tf_op jit(solution)/shard_map/psum | solution.py:15
  1046.9 10.6 all-reduce.6
  1060.6 10.3 all-reduce.3
  (796 shorter events, 434.3 us)
Async XLA Ops:
  34.6 36.5 %all-to-all-start = ((bf16[64,2,1200]{2,1,0:T(2,128)(2,1)}), bf16[64,2,1200]{2,1,0:T(2,128)(2,1)}, u32[]{:S(2)}, u32[]{:S(2)}) async-start(bf16[64,2,1200]{2,1,0:T(2,128)(2,1)} %reshape.628), calls=%async_computation | async-start | bytes 655360 | tf_op jit(solution)/shard_map/all_to_all | solution.py:83
  159.8 38.2 %copy-start.76 = (bf16[1,10,2,12,1,10]{5,3,2,1,4,0:T(8,128)(2,1)S(1)}, bf16[1,10,2,12,1,10]{5,3,2,1,4,0:T(8,128)(2,1)}, u32[]{:S(2)}) copy-start(bf16[1,10,2,12,1,10]{5,3,2,1,4,0:T(8,128)(2,1)} %stack.652) | copy-start | bytes 14404
  159.9 38.9 %copy-start.79 = (bf16[1,10,2,12,1,10]{5,3,2,1,4,0:T(8,128)(2,1)S(1)}, bf16[1,10,2,12,1,10]{5,3,2,1,4,0:T(8,128)(2,1)}, u32[]{:S(2)}) copy-start(bf16[1,10,2,12,1,10]{5,3,2,1,4,0:T(8,128)(2,1)} %stack.653) | copy-start | bytes 14404
  159.9 39.5 %copy-start.82 = (bf16[1,10,2,12,1,10]{5,3,2,1,4,0:T(8,128)(2,1)S(1)}, bf16[1,10,2,12,1,10]{5,3,2,1,4,0:T(8,128)(2,1)}, u32[]{:S(2)}) copy-start(bf16[1,10,2,12,1,10]{5,3,2,1,4,0:T(8,128)(2,1)} %stack.654) | copy-start | bytes 14404
  500.1 37.8 %copy-start.6 = (bf16[1,10,2,12,1,10]{5,3,2,1,4,0:T(8,128)(2,1)S(1)}, bf16[1,10,2,12,1,10]{5,3,2,1,4,0:T(8,128)(2,1)}, u32[]{:S(2)}) copy-start(bf16[1,10,2,12,1,10]{5,3,2,1,4,0:T(8,128)(2,1)} %stack.691) | copy-start | bytes 14404
  500.1 38.4 %copy-start.8 = (bf16[1,10,2,12,1,10]{5,3,2,1,4,0:T(8,128)(2,1)S(1)}, bf16[1,10,2,12,1,10]{5,3,2,1,4,0:T(8,128)(2,1)}, u32[]{:S(2)}) copy-start(bf16[1,10,2,12,1,10]{5,3,2,1,4,0:T(8,128)(2,1)} %stack.692) | copy-start | bytes 14404
  500.1 39.1 %copy-start.10 = (bf16[1,10,2,12,1,10]{5,3,2,1,4,0:T(8,128)(2,1)S(1)}, bf16[1,10,2,12,1,10]{5,3,2,1,4,0:T(8,128)(2,1)}, u32[]{:S(2)}) copy-start(bf16[1,10,2,12,1,10]{5,3,2,1,4,0:T(8,128)(2,1)} %stack.693) | copy-start | bytes 14404
  500.1 39.7 %copy-start.12 = (bf16[1,10,2,12,1,10]{5,3,2,1,4,0:T(8,128)(2,1)S(1)}, bf16[1,10,2,12,1,10]{5,3,2,1,4,0:T(8,128)(2,1)}, u32[]{:S(2)}) copy-start(bf16[1,10,2,12,1,10]{5,3,2,1,4,0:T(8,128)(2,1)} %stack.694) | copy-start | bytes 14404
  500.1 40.3 %copy-start.14 = (bf16[1,10,2,12,1,10]{5,3,2,1,4,0:T(8,128)(2,1)S(1)}, bf16[1,10,2,12,1,10]{5,3,2,1,4,0:T(8,128)(2,1)}, u32[]{:S(2)}) copy-start(bf16[1,10,2,12,1,10]{5,3,2,1,4,0:T(8,128)(2,1)} %stack.695) | copy-start | bytes 14404
  500.2 41.0 %copy-start.16 = (bf16[1,10,2,12,1,10]{5,3,2,1,4,0:T(8,128)(2,1)S(1)}, bf16[1,10,2,12,1,10]{5,3,2,1,4,0:T(8,128)(2,1)}, u32[]{:S(2)}) copy-start(bf16[1,10,2,12,1,10]{5,3,2,1,4,0:T(8,128)(2,1)} %stack.696) | copy-start | bytes 14404
  500.2 41.6 %copy-start.18 = (bf16[1,10,2,12,1,10]{5,3,2,1,4,0:T(8,128)(2,1)S(1)}, bf16[1,10,2,12,1,10]{5,3,2,1,4,0:T(8,128)(2,1)}, u32[]{:S(2)}) copy-start(bf16[1,10,2,12,1,10]{5,3,2,1,4,0:T(8,128)(2,1)} %stack.697) | copy-start | bytes 14404
  500.2 42.2 %copy-start.20 = (bf16[1,10,2,12,1,10]{5,3,2,1,4,0:T(8,128)(2,1)S(1)}, bf16[1,10,2,12,1,10]{5,3,2,1,4,0:T(8,128)(2,1)}, u32[]{:S(2)}) copy-start(bf16[1,10,2,12,1,10]{5,3,2,1,4,0:T(8,128)(2,1)} %stack.698) | copy-start | bytes 14404
  500.2 42.8 %copy-start.23 = (bf16[1,10,2,12,1,10]{5,3,2,1,4,0:T(8,128)(2,1)S(1)}, bf16[1,10,2,12,1,10]{5,3,2,1,4,0:T(8,128)(2,1)}, u32[]{:S(2)}) copy-start(bf16[1,10,2,12,1,10]{5,3,2,1,4,0:T(8,128)(2,1)} %stack.699) | copy-start | bytes 14404
  500.2 43.5 %copy-start.26 = (bf16[1,10,2,12,1,10]{5,3,2,1,4,0:T(8,128)(2,1)S(1)}, bf16[1,10,2,12,1,10]{5,3,2,1,4,0:T(8,128)(2,1)}, u32[]{:S(2)}) copy-start(bf16[1,10,2,12,1,10]{5,3,2,1,4,0:T(8,128)(2,1)} %stack.700) | copy-start | bytes 14404
  500.2 44.1 %copy-start.29 = (bf16[1,10,2,12,1,10]{5,3,2,1,4,0:T(8,128)(2,1)S(1)}, bf16[1,10,2,12,1,10]{5,3,2,1,4,0:T(8,128)(2,1)}, u32[]{:S(2)}) copy-start(bf16[1,10,2,12,1,10]{5,3,2,1,4,0:T(8,128)(2,1)} %stack.701) | copy-start | bytes 14404
  500.2 44.7 %copy-start.32 = (bf16[1,10,2,12,1,10]{5,3,2,1,4,0:T(8,128)(2,1)S(1)}, bf16[1,10,2,12,1,10]{5,3,2,1,4,0:T(8,128)(2,1)}, u32[]{:S(2)}) copy-start(bf16[1,10,2,12,1,10]{5,3,2,1,4,0:T(8,128)(2,1)} %stack.702) | copy-start | bytes 14404
  500.2 45.4 %copy-start.35 = (bf16[1,10,2,12,1,10]{5,3,2,1,4,0:T(8,128)(2,1)S(1)}, bf16[1,10,2,12,1,10]{5,3,2,1,4,0:T(8,128)(2,1)}, u32[]{:S(2)}) copy-start(bf16[1,10,2,12,1,10]{5,3,2,1,4,0:T(8,128)(2,1)} %stack.703) | copy-start | bytes 14404
  500.2 46.0 %copy-start.38 = (bf16[1,10,2,12,1,10]{5,3,2,1,4,0:T(8,128)(2,1)S(1)}, bf16[1,10,2,12,1,10]{5,3,2,1,4,0:T(8,128)(2,1)}, u32[]{:S(2)}) copy-start(bf16[1,10,2,12,1,10]{5,3,2,1,4,0:T(8,128)(2,1)} %stack.704) | copy-start | bytes 14404
  500.2 46.6 %copy-start.41 = (bf16[1,10,2,12,1,10]{5,3,2,1,4,0:T(8,128)(2,1)S(1)}, bf16[1,10,2,12,1,10]{5,3,2,1,4,0:T(8,128)(2,1)}, u32[]{:S(2)}) copy-start(bf16[1,10,2,12,1,10]{5,3,2,1,4,0:T(8,128)(2,1)} %stack.705) | copy-start | bytes 14404
  500.3 47.3 %copy-start.44 = (bf16[1,10,2,12,1,10]{5,3,2,1,4,0:T(8,128)(2,1)S(1)}, bf16[1,10,2,12,1,10]{5,3,2,1,4,0:T(8,128)(2,1)}, u32[]{:S(2)}) copy-start(bf16[1,10,2,12,1,10]{5,3,2,1,4,0:T(8,128)(2,1)} %stack.706) | copy-start | bytes 14404
  500.3 47.9 %copy-start.47 = (bf16[1,10,2,12,1,10]{5,3,2,1,4,0:T(8,128)(2,1)S(1)}, bf16[1,10,2,12,1,10]{5,3,2,1,4,0:T(8,128)(2,1)}, u32[]{:S(2)}) copy-start(bf16[1,10,2,12,1,10]{5,3,2,1,4,0:T(8,128)(2,1)} %stack.707) | copy-start | bytes 14404
  500.3 48.5 %copy-start.50 = (bf16[1,10,2,12,1,10]{5,3,2,1,4,0:T(8,128)(2,1)S(1)}, bf16[1,10,2,12,1,10]{5,3,2,1,4,0:T(8,128)(2,1)}, u32[]{:S(2)}) copy-start(bf16[1,10,2,12,1,10]{5,3,2,1,4,0:T(8,128)(2,1)} %stack.708) | copy-start | bytes 14404
  500.3 49.1 %copy-start.53 = (bf16[1,10,2,12,1,10]{5,3,2,1,4,0:T(8,128)(2,1)S(1)}, bf16[1,10,2,12,1,10]{5,3,2,1,4,0:T(8,128)(2,1)}, u32[]{:S(2)}) copy-start(bf16[1,10,2,12,1,10]{5,3,2,1,4,0:T(8,128)(2,1)} %stack.709) | copy-start | bytes 14404
  500.3 49.8 %copy-start.56 = (bf16[1,10,2,12,1,10]{5,3,2,1,4,0:T(8,128)(2,1)S(1)}, bf16[1,10,2,12,1,10]{5,3,2,1,4,0:T(8,128)(2,1)}, u32[]{:S(2)}) copy-start(bf16[1,10,2,12,1,10]{5,3,2,1,4,0:T(8,128)(2,1)} %stack.710) | copy-start | bytes 14404
  500.3 50.4 %copy-start.59 = (bf16[1,10,2,12,1,10]{5,3,2,1,4,0:T(8,128)(2,1)S(1)}, bf16[1,10,2,12,1,10]{5,3,2,1,4,0:T(8,128)(2,1)}, u32[]{:S(2)}) copy-start(bf16[1,10,2,12,1,10]{5,3,2,1,4,0:T(8,128)(2,1)} %stack.711) | copy-start | bytes 14404
  500.3 51.0 %copy-start.62 = (bf16[1,10,2,12,1,10]{5,3,2,1,4,0:T(8,128)(2,1)S(1)}, bf16[1,10,2,12,1,10]{5,3,2,1,4,0:T(8,128)(2,1)}, u32[]{:S(2)}) copy-start(bf16[1,10,2,12,1,10]{5,3,2,1,4,0:T(8,128)(2,1)} %stack.712) | copy-start | bytes 14404
  500.3 51.7 %copy-start.65 = (bf16[1,10,2,12,1,10]{5,3,2,1,4,0:T(8,128)(2,1)S(1)}, bf16[1,10,2,12,1,10]{5,3,2,1,4,0:T(8,128)(2,1)}, u32[]{:S(2)}) copy-start(bf16[1,10,2,12,1,10]{5,3,2,1,4,0:T(8,128)(2,1)} %stack.713) | copy-start | bytes 14404
  500.3 52.3 %copy-start.68 = (bf16[1,10,2,12,1,10]{5,3,2,1,4,0:T(8,128)(2,1)S(1)}, bf16[1,10,2,12,1,10]{5,3,2,1,4,0:T(8,128)(2,1)}, u32[]{:S(2)}) copy-start(bf16[1,10,2,12,1,10]{5,3,2,1,4,0:T(8,128)(2,1)} %stack.714) | copy-start | bytes 14404
  500.3 52.9 %copy-start.71 = (bf16[1,10,2,12,1,10]{5,3,2,1,4,0:T(8,128)(2,1)S(1)}, bf16[1,10,2,12,1,10]{5,3,2,1,4,0:T(8,128)(2,1)}, u32[]{:S(2)}) copy-start(bf16[1,10,2,12,1,10]{5,3,2,1,4,0:T(8,128)(2,1)} %stack.715) | copy-start | bytes 14404
  500.4 53.6 %copy-start.74 = (bf16[1,10,2,12,1,10]{5,3,2,1,4,0:T(8,128)(2,1)S(1)}, bf16[1,10,2,12,1,10]{5,3,2,1,4,0:T(8,128)(2,1)}, u32[]{:S(2)}) copy-start(bf16[1,10,2,12,1,10]{5,3,2,1,4,0:T(8,128)(2,1)} %stack.716) | copy-start | bytes 14404
  500.4 54.2 %copy-start.77 = (bf16[1,10,2,12,1,10]{5,3,2,1,4,0:T(8,128)(2,1)S(1)}, bf16[1,10,2,12,1,10]{5,3,2,1,4,0:T(8,128)(2,1)}, u32[]{:S(2)}) copy-start(bf16[1,10,2,12,1,10]{5,3,2,1,4,0:T(8,128)(2,1)} %stack.717) | copy-start | bytes 14404
  500.4 54.8 %copy-start.80 = (bf16[1,10,2,12,1,10]{5,3,2,1,4,0:T(8,128)(2,1)S(1)}, bf16[1,10,2,12,1,10]{5,3,2,1,4,0:T(8,128)(2,1)}, u32[]{:S(2)}) copy-start(bf16[1,10,2,12,1,10]{5,3,2,1,4,0:T(8,128)(2,1)} %stack.718) | copy-start | bytes 14404
  500.4 55.5 %copy-start.83 = (bf16[1,10,2,12,1,10]{5,3,2,1,4,0:T(8,128)(2,1)S(1)}, bf16[1,10,2,12,1,10]{5,3,2,1,4,0:T(8,128)(2,1)}, u32[]{:S(2)}) copy-start(bf16[1,10,2,12,1,10]{5,3,2,1,4,0:T(8,128)(2,1)} %stack.719) | copy-start | bytes 14404
  881.3 45.4 %copy-start.3 = (bf16[1,10,2,12,1,10]{5,3,2,1,4,0:T(8,128)(2,1)S(1)}, bf16[1,10,2,12,1,10]{5,3,2,1,4,0:T(8,128)(2,1)}, u32[]{:S(2)}) copy-start(bf16[1,10,2,12,1,10]{5,3,2,1,4,0:T(8,128)(2,1)} %stack.754) | copy-start | bytes 14404
  881.3 46.0 %copy-start.5 = (bf16[1,10,2,12,1,10]{5,3,2,1,4,0:T(8,128)(2,1)S(1)}, bf16[1,10,2,12,1,10]{5,3,2,1,4,0:T(8,128)(2,1)}, u32[]{:S(2)}) copy-start(bf16[1,10,2,12,1,10]{5,3,2,1,4,0:T(8,128)(2,1)} %stack.755) | copy-start | bytes 14404
  881.3 46.7 %copy-start.7 = (bf16[1,10,2,12,1,10]{5,3,2,1,4,0:T(8,128)(2,1)S(1)}, bf16[1,10,2,12,1,10]{5,3,2,1,4,0:T(8,128)(2,1)}, u32[]{:S(2)}) copy-start(bf16[1,10,2,12,1,10]{5,3,2,1,4,0:T(8,128)(2,1)} %stack.756) | copy-start | bytes 14404
  881.3 47.3 %copy-start.9 = (bf16[1,10,2,12,1,10]{5,3,2,1,4,0:T(8,128)(2,1)S(1)}, bf16[1,10,2,12,1,10]{5,3,2,1,4,0:T(8,128)(2,1)}, u32[]{:S(2)}) copy-start(bf16[1,10,2,12,1,10]{5,3,2,1,4,0:T(8,128)(2,1)} %stack.757) | copy-start | bytes 14404
  881.3 47.9 %copy-start.11 = (bf16[1,10,2,12,1,10]{5,3,2,1,4,0:T(8,128)(2,1)S(1)}, bf16[1,10,2,12,1,10]{5,3,2,1,4,0:T(8,128)(2,1)}, u32[]{:S(2)}) copy-start(bf16[1,10,2,12,1,10]{5,3,2,1,4,0:T(8,128)(2,1)} %stack.758) | copy-start | bytes 14404
  881.3 48.6 %copy-start.13 = (bf16[1,10,2,12,1,10]{5,3,2,1,4,0:T(8,128)(2,1)S(1)}, bf16[1,10,2,12,1,10]{5,3,2,1,4,0:T(8,128)(2,1)}, u32[]{:S(2)}) copy-start(bf16[1,10,2,12,1,10]{5,3,2,1,4,0:T(8,128)(2,1)} %stack.759) | copy-start | bytes 14404
  881.3 49.2 %copy-start.15 = (bf16[1,10,2,12,1,10]{5,3,2,1,4,0:T(8,128)(2,1)S(1)}, bf16[1,10,2,12,1,10]{5,3,2,1,4,0:T(8,128)(2,1)}, u32[]{:S(2)}) copy-start(bf16[1,10,2,12,1,10]{5,3,2,1,4,0:T(8,128)(2,1)} %stack.760) | copy-start | bytes 14404
  881.3 49.8 %copy-start.17 = (bf16[1,10,2,12,1,10]{5,3,2,1,4,0:T(8,128)(2,1)S(1)}, bf16[1,10,2,12,1,10]{5,3,2,1,4,0:T(8,128)(2,1)}, u32[]{:S(2)}) copy-start(bf16[1,10,2,12,1,10]{5,3,2,1,4,0:T(8,128)(2,1)} %stack.761) | copy-start | bytes 14404
  881.3 50.4 %copy-start.19 = (bf16[1,10,2,12,1,10]{5,3,2,1,4,0:T(8,128)(2,1)S(1)}, bf16[1,10,2,12,1,10]{5,3,2,1,4,0:T(8,128)(2,1)}, u32[]{:S(2)}) copy-start(bf16[1,10,2,12,1,10]{5,3,2,1,4,0:T(8,128)(2,1)} %stack.762) | copy-start | bytes 14404
  881.4 51.1 %copy-start.21 = (bf16[1,10,2,12,1,10]{5,3,2,1,4,0:T(8,128)(2,1)S(1)}, bf16[1,10,2,12,1,10]{5,3,2,1,4,0:T(8,128)(2,1)}, u32[]{:S(2)}) copy-start(bf16[1,10,2,12,1,10]{5,3,2,1,4,0:T(8,128)(2,1)} %stack.763) | copy-start | bytes 14404
  881.4 51.7 %copy-start.24 = (bf16[1,10,2,12,1,10]{5,3,2,1,4,0:T(8,128)(2,1)S(1)}, bf16[1,10,2,12,1,10]{5,3,2,1,4,0:T(8,128)(2,1)}, u32[]{:S(2)}) copy-start(bf16[1,10,2,12,1,10]{5,3,2,1,4,0:T(8,128)(2,1)} %stack.764) | copy-start | bytes 14404
  881.4 52.3 %copy-start.27 = (bf16[1,10,2,12,1,10]{5,3,2,1,4,0:T(8,128)(2,1)S(1)}, bf16[1,10,2,12,1,10]{5,3,2,1,4,0:T(8,128)(2,1)}, u32[]{:S(2)}) copy-start(bf16[1,10,2,12,1,10]{5,3,2,1,4,0:T(8,128)(2,1)} %stack.765) | copy-start | bytes 14404
  881.4 53.0 %copy-start.30 = (bf16[1,10,2,12,1,10]{5,3,2,1,4,0:T(8,128)(2,1)S(1)}, bf16[1,10,2,12,1,10]{5,3,2,1,4,0:T(8,128)(2,1)}, u32[]{:S(2)}) copy-start(bf16[1,10,2,12,1,10]{5,3,2,1,4,0:T(8,128)(2,1)} %stack.766) | copy-start | bytes 14404
  881.4 53.6 %copy-start.33 = (bf16[1,10,2,12,1,10]{5,3,2,1,4,0:T(8,128)(2,1)S(1)}, bf16[1,10,2,12,1,10]{5,3,2,1,4,0:T(8,128)(2,1)}, u32[]{:S(2)}) copy-start(bf16[1,10,2,12,1,10]{5,3,2,1,4,0:T(8,128)(2,1)} %stack.767) | copy-start | bytes 14404
  881.4 54.2 %copy-start.36 = (bf16[1,10,2,12,1,10]{5,3,2,1,4,0:T(8,128)(2,1)S(1)}, bf16[1,10,2,12,1,10]{5,3,2,1,4,0:T(8,128)(2,1)}, u32[]{:S(2)}) copy-start(bf16[1,10,2,12,1,10]{5,3,2,1,4,0:T(8,128)(2,1)} %stack.768) | copy-start | bytes 14404
  881.4 54.9 %copy-start.39 = (bf16[1,10,2,12,1,10]{5,3,2,1,4,0:T(8,128)(2,1)S(1)}, bf16[1,10,2,12,1,10]{5,3,2,1,4,0:T(8,128)(2,1)}, u32[]{:S(2)}) copy-start(bf16[1,10,2,12,1,10]{5,3,2,1,4,0:T(8,128)(2,1)} %stack.769) | copy-start | bytes 14404
  881.4 55.5 %copy-start.42 = (bf16[1,10,2,12,1,10]{5,3,2,1,4,0:T(8,128)(2,1)S(1)}, bf16[1,10,2,12,1,10]{5,3,2,1,4,0:T(8,128)(2,1)}, u32[]{:S(2)}) copy-start(bf16[1,10,2,12,1,10]{5,3,2,1,4,0:T(8,128)(2,1)} %stack.770) | copy-start | bytes 14404
  881.4 56.1 %copy-start.45 = (bf16[1,10,2,12,1,10]{5,3,2,1,4,0:T(8,128)(2,1)S(1)}, bf16[1,10,2,12,1,10]{5,3,2,1,4,0:T(8,128)(2,1)}, u32[]{:S(2)}) copy-start(bf16[1,10,2,12,1,10]{5,3,2,1,4,0:T(8,128)(2,1)} %stack.771) | copy-start | bytes 14404
  881.4 56.7 %copy-start.48 = (bf16[1,10,2,12,1,10]{5,3,2,1,4,0:T(8,128)(2,1)S(1)}, bf16[1,10,2,12,1,10]{5,3,2,1,4,0:T(8,128)(2,1)}, u32[]{:S(2)}) copy-start(bf16[1,10,2,12,1,10]{5,3,2,1,4,0:T(8,128)(2,1)} %stack.772) | copy-start | bytes 14404
  881.5 57.4 %copy-start.51 = (bf16[1,10,2,12,1,10]{5,3,2,1,4,0:T(8,128)(2,1)S(1)}, bf16[1,10,2,12,1,10]{5,3,2,1,4,0:T(8,128)(2,1)}, u32[]{:S(2)}) copy-start(bf16[1,10,2,12,1,10]{5,3,2,1,4,0:T(8,128)(2,1)} %stack.773) | copy-start | bytes 14404
  881.5 58.0 %copy-start.54 = (bf16[1,10,2,12,1,10]{5,3,2,1,4,0:T(8,128)(2,1)S(1)}, bf16[1,10,2,12,1,10]{5,3,2,1,4,0:T(8,128)(2,1)}, u32[]{:S(2)}) copy-start(bf16[1,10,2,12,1,10]{5,3,2,1,4,0:T(8,128)(2,1)} %stack.774) | copy-start | bytes 14404
  881.5 58.6 %copy-start.57 = (bf16[1,10,2,12,1,10]{5,3,2,1,4,0:T(8,128)(2,1)S(1)}, bf16[1,10,2,12,1,10]{5,3,2,1,4,0:T(8,128)(2,1)}, u32[]{:S(2)}) copy-start(bf16[1,10,2,12,1,10]{5,3,2,1,4,0:T(8,128)(2,1)} %stack.775) | copy-start | bytes 14404
  881.5 59.3 %copy-start.60 = (bf16[1,10,2,12,1,10]{5,3,2,1,4,0:T(8,128)(2,1)S(1)}, bf16[1,10,2,12,1,10]{5,3,2,1,4,0:T(8,128)(2,1)}, u32[]{:S(2)}) copy-start(bf16[1,10,2,12,1,10]{5,3,2,1,4,0:T(8,128)(2,1)} %stack.776) | copy-start | bytes 14404
  881.5 59.9 %copy-start.63 = (bf16[1,10,2,12,1,10]{5,3,2,1,4,0:T(8,128)(2,1)S(1)}, bf16[1,10,2,12,1,10]{5,3,2,1,4,0:T(8,128)(2,1)}, u32[]{:S(2)}) copy-start(bf16[1,10,2,12,1,10]{5,3,2,1,4,0:T(8,128)(2,1)} %stack.777) | copy-start | bytes 14404
  881.5 60.5 %copy-start.66 = (bf16[1,10,2,12,1,10]{5,3,2,1,4,0:T(8,128)(2,1)S(1)}, bf16[1,10,2,12,1,10]{5,3,2,1,4,0:T(8,128)(2,1)}, u32[]{:S(2)}) copy-start(bf16[1,10,2,12,1,10]{5,3,2,1,4,0:T(8,128)(2,1)} %stack.778) | copy-start | bytes 14404
  881.5 61.2 %copy-start.69 = (bf16[1,10,2,12,1,10]{5,3,2,1,4,0:T(8,128)(2,1)S(1)}, bf16[1,10,2,12,1,10]{5,3,2,1,4,0:T(8,128)(2,1)}, u32[]{:S(2)}) copy-start(bf16[1,10,2,12,1,10]{5,3,2,1,4,0:T(8,128)(2,1)} %stack.779) | copy-start | bytes 14404
  881.5 61.8 %copy-start.72 = (bf16[1,10,2,12,1,10]{5,3,2,1,4,0:T(8,128)(2,1)S(1)}, bf16[1,10,2,12,1,10]{5,3,2,1,4,0:T(8,128)(2,1)}, u32[]{:S(2)}) copy-start(bf16[1,10,2,12,1,10]{5,3,2,1,4,0:T(8,128)(2,1)} %stack.780) | copy-start | bytes 14404
  881.5 62.4 %copy-start.75 = (bf16[1,10,2,12,1,10]{5,3,2,1,4,0:T(8,128)(2,1)S(1)}, bf16[1,10,2,12,1,10]{5,3,2,1,4,0:T(8,128)(2,1)}, u32[]{:S(2)}) copy-start(bf16[1,10,2,12,1,10]{5,3,2,1,4,0:T(8,128)(2,1)} %stack.781) | copy-start | bytes 14404
  881.5 63.1 %copy-start.78 = (bf16[1,10,2,12,1,10]{5,3,2,1,4,0:T(8,128)(2,1)S(1)}, bf16[1,10,2,12,1,10]{5,3,2,1,4,0:T(8,128)(2,1)}, u32[]{:S(2)}) copy-start(bf16[1,10,2,12,1,10]{5,3,2,1,4,0:T(8,128)(2,1)} %stack.782) | copy-start | bytes 14404
  881.6 63.7 %copy-start.81 = (bf16[1,10,2,12,1,10]{5,3,2,1,4,0:T(8,128)(2,1)S(1)}, bf16[1,10,2,12,1,10]{5,3,2,1,4,0:T(8,128)(2,1)}, u32[]{:S(2)}) copy-start(bf16[1,10,2,12,1,10]{5,3,2,1,4,0:T(8,128)(2,1)} %stack.783) | copy-start | bytes 14404
  881.6 64.3 %copy-start.84 = (bf16[1,10,2,12,1,10]{5,3,2,1,4,0:T(8,128)(2,1)S(1)}, bf16[1,10,2,12,1,10]{5,3,2,1,4,0:T(8,128)(2,1)}, u32[]{:S(2)}) copy-start(bf16[1,10,2,12,1,10]{5,3,2,1,4,0:T(8,128)(2,1)} %stack.784) | copy-start | bytes 14404
  (26 other events, 745.3 us)
